TPU v7x, 32 devices: a whole 2x2x4 slice. The times are simulated.
32 devices in a mesh: col: 8 (over y, x, core), row: 4 (over z).
Axes of the slice: x: 2, y: 2, z: 4, core: 2. Of those that a mesh axis runs over, the one named last changes fastest.
Arguments:
- trace_start: float32 [32, 32768], P(None, ('col', 'row')), may hold values from -6 to 6
- surface_load: float32 [32, 32768], P(None, ('col', 'row')), may hold values from -6 to 6
- panel_tiles: bfloat16 [704, 512, 512], P(('col', 'row')), may hold values from -0.03125 to 0.03125
- tile_list: int32 [704], P(('col', 'row')), may hold values from -1 to 4095, as said below
- surf_map: int32 [8], replicated, may hold values from 0 to 7, as said below
- coef_index: int32 [2, 4, 16384], P(None, None, 'row'), may hold values from 0 to 15
- coef_table: float32 [16], replicated, may hold values from 0.2 to 2
- vol_source: float32 [2, 4, 16384], P(None, None, 'row'), may hold values from -6 to 6
Outputs:
- traces: float32 [32, 32768], P(None, ('col', 'row'))
- response: float32 [32, 32768], P(None, ('col', 'row'))
Inputs may be any that keep to these rules, and one draw needn't show every extreme that they name: `tile_list`: each device has 22 slots, ordered by col index, then row index, then slot. A value i * 64 + j names the tile of rows i * 512 to (i + 1) * 512 - 1 and columns j * 512 to (j + 1) * 512 - 1 of the boundary matrix, with j <= i and j < 8; each such tile is named exactly once. A device of col index c and row index r names only tiles whose rows lie in shards of row index r (i * 512 // 1024 leaves remainder r modulo 4), and none if c >= 6; its named tiles fill its first slots and the rest hold -1. Some device names 22 tiles. surf_map[r * 2 + q] leaves remainder r modulo 4; each volume tile lies under exactly one surface tile.
All inputs are finite; a program needn't handle non-finite values.
Results may differ from a plain program's by a relative error of at most 0.0041.
Values may be sent and summed in bfloat16 or wider, within the bound.
A program may use at most 128 MiB of HBM per device.

v0:
```python
import jax
import jax.numpy as jnp
from jax import lax
from jax.sharding import PartitionSpec as P

ITERS = 2
SWEEPS = 4


COUPLING_STEP = 0.3
JACOBI_WEIGHT = 0.8
CELL_MASS = 0.05


def padded(x, sides, width):
    for axis, dim in sides:
        peers, length = (lax.axis_size(axis), x.shape[dim])
        up = [(i, (i + 1) % peers) for i in range(peers - 1)]
        down = [(j, i) for i, j in up]
        last = lax.slice_in_dim(x, length - width, length, axis=dim)
        first = lax.slice_in_dim(x, 0, width, axis=dim)
        before = lax.ppermute(last, axis, up)
        after = lax.ppermute(first, axis, down)
        x = jnp.concatenate([before, x, after], axis=dim)
    return x


def lookup_coefs(indices, coef_values):
    levels = jnp.arange(coef_values.shape[0], dtype=jnp.int32)
    return jnp.sum(jnp.where(indices[..., None] == levels, coef_values, 0.0), axis=-1)


def relax_line(padded_values, coefs_pad, source, top_trace):
    centre_coef = coefs_pad[:, 1:-1]
    left_weight = 0.5 * (centre_coef + coefs_pad[:, :-2])
    right_weight = 0.5 * (centre_coef + coefs_pad[:, 2:])
    layer_weight = 0.5 * (centre_coef[:-1] + centre_coef[1:])
    upper_weight = jnp.concatenate([centre_coef[:1], layer_weight], 0)
    lower_weight = jnp.concatenate([layer_weight, jnp.zeros_like(centre_coef[:1])], 0)
    centre = padded_values[:, :, 1:-1]
    upper_values = jnp.concatenate([top_trace[:, None, :], centre[:, :-1]], 1)
    lower_values = jnp.concatenate([centre[:, 1:], jnp.zeros_like(centre[:, :1])], 1)
    gathered = (
        left_weight * padded_values[:, :, :-2]
        + right_weight * padded_values[:, :, 2:]
        + upper_weight * upper_values
        + lower_weight * lower_values
        + source
    )
    diagonal = left_weight + right_weight + upper_weight + lower_weight + CELL_MASS
    return (1.0 - JACOBI_WEIGHT) * centre + JACOBI_WEIGHT * gathered / diagonal


def add_block(partial_value, block_sum, block_start):
    current = lax.dynamic_slice_in_dim(partial_value, block_start, block_sum.shape[1], 1)
    return lax.dynamic_update_slice_in_dim(partial_value, current + block_sum, block_start, 1)


def apply_slots(panel_part, ident_part, band_traces, window_traces, row_count):
    rhs_count = band_traces.shape[0]
    tile_width = panel_part.shape[1]
    shard_width = window_traces.shape[1] // row_count
    per_shard = shard_width // tile_width
    tiles_side = band_traces.shape[1] * row_count // tile_width
    band_tiles = band_traces.shape[1] // tile_width
    window_tiles = window_traces.shape[1] // tile_width
    is_valid = ident_part >= 0
    safe_ident = jnp.where(is_valid, ident_part, 0)
    row_tile = safe_ident // tiles_side
    col_tile = safe_ident % tiles_side
    shard_number = row_tile // per_shard
    band_tile = shard_number // row_count * per_shard + row_tile % per_shard
    band_blocks = band_traces.reshape(rhs_count, band_tiles, tile_width)
    window_blocks = window_traces.reshape(rhs_count, window_tiles, tile_width)
    row_parts = jnp.take(band_blocks, band_tile, axis=1)
    col_parts = jnp.take(window_blocks, col_tile, axis=1)
    into_rows = jnp.einsum(
        "rsk,sjk->srj", col_parts, panel_part, preferred_element_type=jnp.float32
    )
    into_cols = jnp.einsum(
        "rsk,skj->srj", row_parts, panel_part, preferred_element_type=jnp.float32
    )
    valid_weight = is_valid.astype(jnp.float32)[:, None]
    band_onehot = (band_tile[:, None] == jnp.arange(band_tiles, dtype=jnp.int32)[None, :]).astype(
        jnp.float32
    ) * valid_weight
    window_onehot = (
        col_tile[:, None] == jnp.arange(window_tiles, dtype=jnp.int32)[None, :]
    ).astype(jnp.float32) * valid_weight
    band_add = jnp.einsum("srj,sb->rbj", into_rows, band_onehot, precision=lax.Precision.HIGHEST)
    window_add = jnp.einsum(
        "srj,sb->rbj", into_cols, window_onehot, precision=lax.Precision.HIGHEST
    )
    return (band_add.reshape(rhs_count, -1), window_add.reshape(rhs_count, -1))


def sweep_volume(volume_state, coefs_pad, line_source, top_trace):
    for sweep_index in range(SWEEPS):
        padded_state = padded(volume_state, (("row", 2),), 1)
        volume_state = relax_line(padded_state, coefs_pad, line_source, top_trace)
    return volume_state


def local(
    trace_start, surface_load, panel_tiles, tile_list, surf_map, coef_index, coef_table, vol_source
):
    column_count = lax.axis_size("col")
    row_count = lax.axis_size("row")
    volume_count = column_count // 4
    dense_count = column_count - volume_count
    col_index = lax.axis_index("col")
    row_index = lax.axis_index("row")
    volume_line = jnp.maximum(col_index - dense_count, 0)
    is_volume = col_index >= dense_count
    line_coefs = lookup_coefs(
        lax.dynamic_index_in_dim(coef_index, volume_line, 0, keepdims=False), coef_table
    )
    line_source = lax.dynamic_index_in_dim(vol_source, volume_line, 0, keepdims=False)
    coefs_pad = padded(line_coefs, (("row", 1),), 1)
    volume_tile = volume_line * row_count + row_index
    tile_numbers = jnp.arange(surf_map.shape[0], dtype=jnp.int32)
    surface_tile = jnp.sum(jnp.where(surf_map == volume_tile, tile_numbers, 0))
    node_count = line_coefs.shape[1]
    flux_start = surface_tile % volume_count * node_count
    rhs_count = trace_start.shape[0]
    shard_width = trace_start.shape[1]
    band_width = shard_width * column_count
    window_width = shard_width * row_count
    volume_state = jnp.zeros((rhs_count, line_coefs.shape[0], node_count), jnp.float32)
    work_lists = (panel_tiles, tile_list)
    traces = trace_start
    response = trace_start
    for iteration in range(ITERS):
        band_traces = lax.all_gather(traces.astype(jnp.bfloat16), "col", axis=1, tiled=True)
        window_traces = lax.all_gather(band_traces[:, :shard_width], "row", axis=1, tiled=True)
        partials = (
            jnp.zeros((rhs_count, band_width), jnp.float32),
            jnp.zeros((rhs_count, window_width), jnp.float32),
        )
        panel_part, ident_part = work_lists
        partials = apply_slots(panel_part, ident_part, band_traces, window_traces, row_count)
        band_partial, window_partial = partials
        top_trace = lax.dynamic_slice_in_dim(band_traces, flux_start, node_count, 1).astype(
            jnp.float32
        )
        volume_state = sweep_volume(volume_state, coefs_pad, line_source, top_trace)
        top_flux = jnp.where(is_volume, line_coefs[0] * (top_trace - volume_state[:, 0]), 0.0)
        band_partial = add_block(band_partial, top_flux, flux_start)
        window_share = lax.psum_scatter(window_partial, "row", scatter_dimension=1, tiled=True)
        band_partial = add_block(band_partial, window_share, 0)
        response = lax.psum_scatter(band_partial, "col", scatter_dimension=1, tiled=True)
        traces = traces + COUPLING_STEP * (surface_load - traces - response)
    return (traces, response)


def solution(mesh):
    return jax.shard_map(
        local,
        mesh=mesh,
        in_specs=(
            P(None, ("col", "row")),
            P(None, ("col", "row")),
            P(("col", "row"), None, None),
            P(("col", "row")),
            P(),
            P(None, None, "row"),
            P(),
            P(None, None, "row"),
        ),
        out_specs=(P(None, ("col", "row")), P(None, ("col", "row"))),
        check_vma=False,
    )
```

profile of v0, /device:TPU:1, one launch (start us, length us, event | category | flops | bytes accessed | tf_op | source)
XLA Modules:
  0.0 277.9 jit_solution(6785955184059688862)
XLA Ops:
  7.2 4.0 %collective-permute-start.1 = (f32[32,4,1]{2,0,1:T(8,128)S(1)}, f32[32,4,1]{2,0,1:T(8,128)S(1)}, u32[]{:S(2)}, u32[]{:S(2)}) collective-permute-start(f32[32,4,1]{2,0,1:T(8,128)S(1)} %broadcast.137), channel_id=1, source_target_pairs={{0,1},{1,2},{2,3},{4,5},{5,6},{6,7},{8,9},{9,10},{10,11},{12,13},{... | collective-permute-start | bytes 1544 | tf_op jit(solution)/shard_map/ppermute | solution.py:22
  14.9 4.6 %collective-permute-start = (f32[4,1]{1,0:T(4,128)S(1)}, f32[4,1]{1,0:T(4,128)S(1)}, u32[]{:S(2)}, u32[]{:S(2)}) collective-permute-start(f32[4,1]{1,0:T(4,128)S(1)} %get-tuple-element.42), channel_id=1, source_target_pairs={{0,1},{1,2},{2,3},{4,5},{5,6},{6,7},{8,9},{9,10},{10,11},{12,13},{... | collective-permute-start | bytes 56 | tf_op jit(solution)/shard_map/ppermute | solution.py:22
  20.5 11.2 %all_gather.12 = bf16[32,8192]{1,0:T(8,128)(2,1)S(1)} all-gather(bf16[32,1024]{1,0:T(8,128)(2,1)S(1)} %convert_element_type.21), channel_id=1, replica_groups=mesh['col'=8,'row'=4] {'col'}, dimensions={1}, use_global_device_ids=true | all-gather | bytes 589824 | tf_op jit(solution)/shard_map/all_gather | solution.py:134
  33.1 6.4 %fusion.84 = f32[22,32,512]{2,1,0:T(8,128)S(1)} fusion(bf16[22,512,512]{2,1,0:T(8,128)(2,1)} %param.14, bf16[22,32,512]{2,1,0:T(8,128)(2,1)S(1)} %gather_fusion.1, pred[22]{0:T(512)(128)(4,1)S(1)} %get-tuple-element.4), kind=kOutput, calls=%fused_computation.113 | convolution fusion | flops 369459200 | bytes 13697046 | tf_op jit(solution)/shard_map/rsk,skj->srj/dot_general | solution.py:80
  45.2 14.1 %all_gather.13 = bf16[32,4096]{1,0:T(8,128)(2,1)S(1)} all-gather(bf16[32,1024]{1,0:T(8,128)(2,1)S(1)} %slice.283), channel_id=1, replica_groups=mesh['col'=8,'row'=4] {'row'}, dimensions={1}, use_global_device_ids=true | all-gather | bytes 327680 | tf_op jit(solution)/shard_map/all_gather | solution.py:135
  60.0 7.8 %fusion.86 = f32[22,32,512]{2,1,0:T(8,128)S(1)} fusion(bf16[22,512,512]{2,1,0:T(8,128)(2,1)} %param.14, bf16[22,32,512]{2,1,0:T(8,128)(2,1)S(1)} %gather_fusion, pred[22]{0:T(512)(128)(4,1)S(1)} %get-tuple-element.11), kind=kOutput, calls=%fused_computation.115 | convolution fusion | flops 369459200 | bytes 13697046 | tf_op jit(solution)/shard_map/rsk,sjk->srj/dot_general | solution.py:77
  73.4 4.0 %collective-permute-start.4 = (f32[32,4,1]{2,0,1:T(8,128)S(1)}, f32[32,4,1]{2,0,1:T(8,128)S(1)}, u32[]{:S(2)}, u32[]{:S(2)}) collective-permute-start(f32[32,4,1]{2,0,1:T(8,128)S(1)} %get-tuple-element.39), channel_id=1, source_target_pairs={{0,1},{1,2},{2,3},{4,5},{5,6},{6,7},{8,9},{9,10},{10,11},{12,13},{... | collective-permute-start | bytes 1544 | tf_op jit(solution)/shard_map/ppermute | solution.py:22
  82.3 4.3 %collective-permute-start.6 = (f32[32,4,1]{2,0,1:T(8,128)S(1)}, f32[32,4,1]{2,0,1:T(8,128)S(1)}, u32[]{:S(2)}, u32[]{:S(2)}) collective-permute-start(f32[32,4,1]{2,0,1:T(8,128)S(1)} %get-tuple-element.35), channel_id=1, source_target_pairs={{0,1},{1,2},{2,3},{4,5},{5,6},{6,7},{8,9},{9,10},{10,11},{12,13},{... | collective-permute-start | bytes 1544 | tf_op jit(solution)/shard_map/ppermute | solution.py:22
  91.4 4.3 %collective-permute-start.8 = (f32[32,4,1]{2,0,1:T(8,128)S(1)}, f32[32,4,1]{2,0,1:T(8,128)S(1)}, u32[]{:S(2)}, u32[]{:S(2)}) collective-permute-start(f32[32,4,1]{2,0,1:T(8,128)S(1)} %get-tuple-element.31), channel_id=1, source_target_pairs={{0,1},{1,2},{2,3},{4,5},{5,6},{6,7},{8,9},{9,10},{10,11},{12,13},{... | collective-permute-start | bytes 1544 | tf_op jit(solution)/shard_map/ppermute | solution.py:22
  106.1 5.0 %collective-permute-start.10 = (f32[32,4,1]{2,0,1:T(8,128)}, f32[32,4,1]{2,0,1:T(8,128)}, u32[]{:S(2)}, u32[]{:S(2)}) collective-permute-start(f32[32,4,1]{2,0,1:T(8,128)} %get-tuple-element.27), channel_id=1, source_target_pairs={{0,1},{1,2},{2,3},{4,5},{5,6},{6,7},{8,9},{9,10},{10,11},{12,13},{... | collective-permute-start | bytes 1544 | tf_op jit(solution)/shard_map/ppermute | solution.py:22
  111.1 2.1 fusion.161
  113.3 32.0 %reduce-scatter.7.cloned.1.call-done = f32[32,1024]{1,0:T(8,128)} async-done(((f32[32,8192]{1,0:T(8,128)}), f32[32,1024]{1,0:T(8,128)}) %reduce-scatter.7.cloned.1.call-update) | async-done | bytes 131088 | tf_op jit(solution)/shard_map/reduce_scatter | solution.py:151
  146.3 10.7 %all_gather.14 = bf16[32,8192]{1,0:T(8,128)(2,1)S(1)} all-gather(bf16[32,1024]{1,0:T(8,128)(2,1)S(1)} %fusion.121), channel_id=1, replica_groups=mesh['col'=8,'row'=4] {'col'}, dimensions={1}, use_global_device_ids=true | all-gather | bytes 589824 | tf_op jit(solution)/shard_map/all_gather | solution.py:134
  157.1 3.3 %fusion.35 = f32[32,4,4096]{2,0,1:T(8,128)S(1)} fusion(f32[32,1,4096]{2,0,1:T(8,128)S(1)} %convert_bitcast_fusion, f32[32,4,1]{2,0,1:T(8,128)} %collective-permute-done.11, f32[32,4,4096]{2,0,1:T(8,128)S(1)} %fusion.28, f32[32,4,1]{2,0,1:T(8,128)} %collective-permute-done.10, f32[32,3,4096]{2,0,1:T(8,128)} %get-tuple-element.26, ...), kind=kLoop, calls=%fused_computation.48 | loop fusion | flops 7864320 | bytes 8258560 | tf_op jit(solution)/shard_map/add | solution.py:51
  163.3 12.1 %all_gather.15 = bf16[32,4096]{1,0:T(8,128)(2,1)S(1)} all-gather(bf16[32,1024]{1,0:T(8,128)(2,1)S(1)} %slice-done), channel_id=1, replica_groups=mesh['col'=8,'row'=4] {'row'}, dimensions={1}, use_global_device_ids=true | all-gather | bytes 327680 | tf_op jit(solution)/shard_map/all_gather | solution.py:135
  176.1 7.7 %fusion.82 = f32[22,32,512]{2,1,0:T(8,128)S(1)} fusion(bf16[22,512,512]{2,1,0:T(8,128)(2,1)} %param.14, bf16[22,32,512]{2,1,0:T(8,128)(2,1)S(1)} %gather_fusion.2, pred[22]{0:T(512)(128)(4,1)S(1)} %copy-done.30), kind=kOutput, calls=%fused_computation.111 | convolution fusion | flops 369459200 | bytes 13697046 | tf_op jit(solution)/shard_map/rsk,sjk->srj/dot_general | solution.py:77
  183.9 2.9 %fusion.74 = f32[16,32,512]{2,0,1:T(8,128)} fusion(f32[22,32,512]{2,1,0:T(8,128)S(1)} %fusion.82, f32[22]{0:T(128)S(1)} %copy-done.24, s32[22]{0:T(128)S(1)} %copy-done.28), kind=kOutput, calls=%fused_computation.101 | convolution fusion | flops 69206720 | bytes 2490544 | tf_op jit(solution)/shard_map/srj,sb->rbj/dot_general | solution.py:90
  188.0 4.6 %collective-permute-start.12 = (f32[32,4,1]{2,0,1:T(8,128)}, f32[32,4,1]{2,0,1:T(8,128)}, u32[]{:S(2)}, u32[]{:S(2)}) collective-permute-start(f32[32,4,1]{2,0,1:T(8,128)} %get-tuple-element.23), channel_id=1, source_target_pairs={{0,1},{1,2},{2,3},{4,5},{5,6},{6,7},{8,9},{9,10},{10,11},{12,13},{... | collective-permute-start | bytes 1544 | tf_op jit(solution)/shard_map/ppermute | solution.py:22
  193.5 6.4 %fusion.80 = f32[22,32,512]{2,1,0:T(8,128)S(1)} fusion(bf16[22,512,512]{2,1,0:T(8,128)(2,1)} %param.14, bf16[22,32,512]{2,1,0:T(8,128)(2,1)S(1)} %gather_fusion.3, pred[22]{0:T(512)(128)(4,1)S(1)} %copy-done.21), kind=kOutput, calls=%fused_computation.109 | convolution fusion | flops 369459200 | bytes 13697046 | tf_op jit(solution)/shard_map/rsk,skj->srj/dot_general | solution.py:80
  204.4 3.4 %fusion.42 = f32[32,4,4096]{2,0,1:T(8,128)S(1)} fusion(f32[32,1,4096]{2,0,1:T(8,128)S(1)} %convert_bitcast_fusion, f32[32,4,1]{2,0,1:T(8,128)} %collective-permute-done.13, f32[32,4,4096]{2,0,1:T(8,128)S(1)} %copy-done.3, f32[32,4,1]{2,0,1:T(8,128)} %collective-permute-done.12, f32[32,3,4096]{2,0,1:T(8,128)} %get-tuple-element.22, ...), kind=kLoop, calls=%fused_computation.55 | loop fusion | flops 7864320 | bytes 8258560 | tf_op jit(solution)/shard_map/add | solution.py:51
  209.2 4.0 %collective-permute-start.14 = (f32[32,4,1]{2,0,1:T(8,128)S(1)}, f32[32,4,1]{2,0,1:T(8,128)S(1)}, u32[]{:S(2)}, u32[]{:S(2)}) collective-permute-start(f32[32,4,1]{2,0,1:T(8,128)S(1)} %get-tuple-element.19), channel_id=1, source_target_pairs={{0,1},{1,2},{2,3},{4,5},{5,6},{6,7},{8,9},{9,10},{10,11},{12,13},{... | collective-permute-start | bytes 1544 | tf_op jit(solution)/shard_map/ppermute | solution.py:22
  214.8 2.1 fusion.49
  218.4 4.7 %collective-permute-start.16 = (f32[32,4,1]{2,0,1:T(8,128)S(1)}, f32[32,4,1]{2,0,1:T(8,128)S(1)}, u32[]{:S(2)}, u32[]{:S(2)}) collective-permute-start(f32[32,4,1]{2,0,1:T(8,128)S(1)} %get-tuple-element.13), channel_id=1, source_target_pairs={{0,1},{1,2},{2,3},{4,5},{5,6},{6,7},{8,9},{9,10},{10,11},{12,13},{... | collective-permute-start | bytes 1544 | tf_op jit(solution)/shard_map/ppermute | solution.py:22
  228.1 41.7 %reduce-scatter.11.cloned.1.call-done = f32[32,1024]{1,0:T(8,128)} async-done(((f32[32,8192]{1,0:T(8,128)}), f32[32,1024]{1,0:T(8,128)}) %reduce-scatter.11.cloned.1.call-update) | async-done | bytes 131088 | tf_op jit(solution)/shard_map/reduce_scatter | solution.py:151
  (172 shorter events, 57.7 us)
Async XLA Ops:
  7.2 93.9 %reduce-scatter.5.cloned.1.call-start = ((), (), s32[]{:S(2)}) async-start(), calls=%async_computation.4 | async-start | bytes 655360 | tf_op jit(solution)/shard_map/reduce_scatter | solution.py:149
  7.2 64.3 %collective-permute-start.1 = (f32[32,4,1]{2,0,1:T(8,128)S(1)}, f32[32,4,1]{2,0,1:T(8,128)S(1)}, u32[]{:S(2)}, u32[]{:S(2)}) collective-permute-start(f32[32,4,1]{2,0,1:T(8,128)S(1)} %broadcast.137), channel_id=1, source_target_pairs={{0,1},{1,2},{2,3},{4,5},{5,6},{6,7},{8,9},{9,10},{10,11},{12,13},{... | collective-permute-start | bytes 1544 | tf_op jit(solution)/shard_map/ppermute | solution.py:22
  11.3 60.3 %collective-permute-start.3 = (f32[32,4,1]{2,0,1:T(8,128)S(1)}, f32[32,4,1]{2,0,1:T(8,128)S(1)}, u32[]{:S(2)}, u32[]{:S(2)}) collective-permute-start(f32[32,4,1]{2,0,1:T(8,128)S(1)} %broadcast.137), channel_id=1, source_target_pairs={{1,0},{2,1},{3,2},{5,4},{6,5},{7,6},{9,8},{10,9},{11,10},{13,12},{... | collective-permute-start | bytes 1544 | tf_op jit(solution)/shard_map/ppermute | solution.py:23
  13.6 57.7 %collective-permute-start.2 = (f32[4,1]{1,0:T(4,128)S(1)}, f32[4,1]{1,0:T(4,128)S(1)}, u32[]{:S(2)}, u32[]{:S(2)}) collective-permute-start(f32[4,1]{1,0:T(4,128)S(1)} %get-tuple-element.43), channel_id=1, source_target_pairs={{1,0},{2,1},{3,2},{5,4},{6,5},{7,6},{9,8},{10,9},{11,10},{13,12},{... | collective-permute-start | bytes 56 | tf_op jit(solution)/shard_map/ppermute | solution.py:23
  14.9 56.4 %collective-permute-start = (f32[4,1]{1,0:T(4,128)S(1)}, f32[4,1]{1,0:T(4,128)S(1)}, u32[]{:S(2)}, u32[]{:S(2)}) collective-permute-start(f32[4,1]{1,0:T(4,128)S(1)} %get-tuple-element.42), channel_id=1, source_target_pairs={{0,1},{1,2},{2,3},{4,5},{5,6},{6,7},{8,9},{9,10},{10,11},{12,13},{... | collective-permute-start | bytes 56 | tf_op jit(solution)/shard_map/ppermute | solution.py:22
  42.4 102.8 %reduce-scatter.7.cloned.1.call-start = ((), (), s32[]{:S(2)}) async-start(), calls=%async_computation.5 | async-start | bytes 1179648 | tf_op jit(solution)/shard_map/reduce_scatter | solution.py:151
  71.3 143.5 %copy-start.9 = (f32[4,4096]{1,0:T(4,128)}, f32[4,4096]{1,0:T(4,128)S(1)}, u32[]{:S(2)}) copy-start(f32[4,4096]{1,0:T(4,128)S(1)} %dynamic-slice_bitcast_fusion) | copy-start | bytes 196612
  72.1 5.6 %collective-permute-start.5 = (f32[32,4,1]{2,0,1:T(8,128)S(1)}, f32[32,4,1]{2,0,1:T(8,128)S(1)}, u32[]{:S(2)}, u32[]{:S(2)}) collective-permute-start(f32[32,4,1]{2,0,1:T(8,128)S(1)} %get-tuple-element.40), channel_id=1, source_target_pairs={{1,0},{2,1},{3,2},{5,4},{6,5},{7,6},{9,8},{10,9},{11,10},{13,12},{... | collective-permute-start | bytes 1544 | tf_op jit(solution)/shard_map/ppermute | solution.py:23
  73.4 5.3 %collective-permute-start.4 = (f32[32,4,1]{2,0,1:T(8,128)S(1)}, f32[32,4,1]{2,0,1:T(8,128)S(1)}, u32[]{:S(2)}, u32[]{:S(2)}) collective-permute-start(f32[32,4,1]{2,0,1:T(8,128)S(1)} %get-tuple-element.39), channel_id=1, source_target_pairs={{0,1},{1,2},{2,3},{4,5},{5,6},{6,7},{8,9},{9,10},{10,11},{12,13},{... | collective-permute-start | bytes 1544 | tf_op jit(solution)/shard_map/ppermute | solution.py:22
  80.8 6.1 %collective-permute-start.7 = (f32[32,4,1]{2,0,1:T(8,128)S(1)}, f32[32,4,1]{2,0,1:T(8,128)S(1)}, u32[]{:S(2)}, u32[]{:S(2)}) collective-permute-start(f32[32,4,1]{2,0,1:T(8,128)S(1)} %get-tuple-element.36), channel_id=1, source_target_pairs={{1,0},{2,1},{3,2},{5,4},{6,5},{7,6},{9,8},{10,9},{11,10},{13,12},{... | collective-permute-start | bytes 1544 | tf_op jit(solution)/shard_map/ppermute | solution.py:23
  82.3 5.6 %collective-permute-start.6 = (f32[32,4,1]{2,0,1:T(8,128)S(1)}, f32[32,4,1]{2,0,1:T(8,128)S(1)}, u32[]{:S(2)}, u32[]{:S(2)}) collective-permute-start(f32[32,4,1]{2,0,1:T(8,128)S(1)} %get-tuple-element.35), channel_id=1, source_target_pairs={{0,1},{1,2},{2,3},{4,5},{5,6},{6,7},{8,9},{9,10},{10,11},{12,13},{... | collective-permute-start | bytes 1544 | tf_op jit(solution)/shard_map/ppermute | solution.py:22
  90.1 6.0 %collective-permute-start.9 = (f32[32,4,1]{2,0,1:T(8,128)S(1)}, f32[32,4,1]{2,0,1:T(8,128)S(1)}, u32[]{:S(2)}, u32[]{:S(2)}) collective-permute-start(f32[32,4,1]{2,0,1:T(8,128)S(1)} %get-tuple-element.32), channel_id=1, source_target_pairs={{1,0},{2,1},{3,2},{5,4},{6,5},{7,6},{9,8},{10,9},{11,10},{13,12},{... | collective-permute-start | bytes 1544 | tf_op jit(solution)/shard_map/ppermute | solution.py:23
  91.4 5.6 %collective-permute-start.8 = (f32[32,4,1]{2,0,1:T(8,128)S(1)}, f32[32,4,1]{2,0,1:T(8,128)S(1)}, u32[]{:S(2)}, u32[]{:S(2)}) collective-permute-start(f32[32,4,1]{2,0,1:T(8,128)S(1)} %get-tuple-element.31), channel_id=1, source_target_pairs={{0,1},{1,2},{2,3},{4,5},{5,6},{6,7},{8,9},{9,10},{10,11},{12,13},{... | collective-permute-start | bytes 1544 | tf_op jit(solution)/shard_map/ppermute | solution.py:22
  102.8 123.3 %reduce-scatter.9.cloned.1.call-start = ((), (), s32[]{:S(2)}) async-start(), calls=%async_computation.6 | async-start | bytes 655360 | tf_op jit(solution)/shard_map/reduce_scatter | solution.py:149
  104.8 52.3 %collective-permute-start.11 = (f32[32,4,1]{2,0,1:T(8,128)}, f32[32,4,1]{2,0,1:T(8,128)}, u32[]{:S(2)}, u32[]{:S(2)}) collective-permute-start(f32[32,4,1]{2,0,1:T(8,128)} %get-tuple-element.28), channel_id=1, source_target_pairs={{1,0},{2,1},{3,2},{5,4},{6,5},{7,6},{9,8},{10,9},{11,10},{13,12},{... | collective-permute-start | bytes 1544 | tf_op jit(solution)/shard_map/ppermute | solution.py:23
  106.1 51.0 %collective-permute-start.10 = (f32[32,4,1]{2,0,1:T(8,128)}, f32[32,4,1]{2,0,1:T(8,128)}, u32[]{:S(2)}, u32[]{:S(2)}) collective-permute-start(f32[32,4,1]{2,0,1:T(8,128)} %get-tuple-element.27), channel_id=1, source_target_pairs={{0,1},{1,2},{2,3},{4,5},{5,6},{6,7},{8,9},{9,10},{10,11},{12,13},{... | collective-permute-start | bytes 1544 | tf_op jit(solution)/shard_map/ppermute | solution.py:22
  186.7 17.7 %collective-permute-start.13 = (f32[32,4,1]{2,0,1:T(8,128)}, f32[32,4,1]{2,0,1:T(8,128)}, u32[]{:S(2)}, u32[]{:S(2)}) collective-permute-start(f32[32,4,1]{2,0,1:T(8,128)} %get-tuple-element.24), channel_id=1, source_target_pairs={{1,0},{2,1},{3,2},{5,4},{6,5},{7,6},{9,8},{10,9},{11,10},{13,12},{... | collective-permute-start | bytes 1544 | tf_op jit(solution)/shard_map/ppermute | solution.py:23
  188.0 16.4 %collective-permute-start.12 = (f32[32,4,1]{2,0,1:T(8,128)}, f32[32,4,1]{2,0,1:T(8,128)}, u32[]{:S(2)}, u32[]{:S(2)}) collective-permute-start(f32[32,4,1]{2,0,1:T(8,128)} %get-tuple-element.23), channel_id=1, source_target_pairs={{0,1},{1,2},{2,3},{4,5},{5,6},{6,7},{8,9},{9,10},{10,11},{12,13},{... | collective-permute-start | bytes 1544 | tf_op jit(solution)/shard_map/ppermute | solution.py:22
  204.3 65.4 %reduce-scatter.11.cloned.1.call-start = ((), (), s32[]{:S(2)}) async-start(), calls=%async_computation.7 | async-start | bytes 1179648 | tf_op jit(solution)/shard_map/reduce_scatter | solution.py:151
  207.9 5.6 %collective-permute-start.15 = (f32[32,4,1]{2,0,1:T(8,128)S(1)}, f32[32,4,1]{2,0,1:T(8,128)S(1)}, u32[]{:S(2)}, u32[]{:S(2)}) collective-permute-start(f32[32,4,1]{2,0,1:T(8,128)S(1)} %get-tuple-element.20), channel_id=1, source_target_pairs={{1,0},{2,1},{3,2},{5,4},{6,5},{7,6},{9,8},{10,9},{11,10},{13,12},{... | collective-permute-start | bytes 1544 | tf_op jit(solution)/shard_map/ppermute | solution.py:23
  209.2 5.6 %collective-permute-start.14 = (f32[32,4,1]{2,0,1:T(8,128)S(1)}, f32[32,4,1]{2,0,1:T(8,128)S(1)}, u32[]{:S(2)}, u32[]{:S(2)}) collective-permute-start(f32[32,4,1]{2,0,1:T(8,128)S(1)} %get-tuple-element.19), channel_id=1, source_target_pairs={{0,1},{1,2},{2,3},{4,5},{5,6},{6,7},{8,9},{9,10},{10,11},{12,13},{... | collective-permute-start | bytes 1544 | tf_op jit(solution)/shard_map/ppermute | solution.py:22
  217.1 6.4 %collective-permute-start.17 = (f32[32,4,1]{2,0,1:T(8,128)S(1)}, f32[32,4,1]{2,0,1:T(8,128)S(1)}, u32[]{:S(2)}, u32[]{:S(2)}) collective-permute-start(f32[32,4,1]{2,0,1:T(8,128)S(1)} %get-tuple-element.14), channel_id=1, source_target_pairs={{1,0},{2,1},{3,2},{5,4},{6,5},{7,6},{9,8},{10,9},{11,10},{13,12},{... | collective-permute-start | bytes 1544 | tf_op jit(solution)/shard_map/ppermute | solution.py:23
  218.4 6.1 %collective-permute-start.16 = (f32[32,4,1]{2,0,1:T(8,128)S(1)}, f32[32,4,1]{2,0,1:T(8,128)S(1)}, u32[]{:S(2)}, u32[]{:S(2)}) collective-permute-start(f32[32,4,1]{2,0,1:T(8,128)S(1)} %get-tuple-element.13), channel_id=1, source_target_pairs={{0,1},{1,2},{2,3},{4,5},{5,6},{6,7},{8,9},{9,10},{10,11},{12,13},{... | collective-permute-start | bytes 1544 | tf_op jit(solution)/shard_map/ppermute | solution.py:22
  225.7 45.6 %copy-start.1 = (s32[2,4,4096]{2,1,0:T(4,128)S(1)}, s32[2,4,4096]{2,1,0:T(4,128)}, u32[]{:S(2)}) copy-start(s32[2,4,4096]{2,1,0:T(4,128)} %param.17) | copy-start | bytes 393220
  (34 other events, 469.3 us)
Sparse Core Ops, SparseCore 0:
  42.6 20.8 reduce-scatter.4
  102.9 42.3 reduce-scatter.6
  204.5 20.9 reduce-scatter.8
  229.1 40.5 reduce-scatter.10
where the time goes:
time: 280 us; the launch traced here: 278 us
  waiting for transfers between devices  79 us (28%)
  starting transfers between devices  51.5 us (18%)
  blocking collectives  48.1 us (17%)
  matrix products  36.5 us (13%)
  other arithmetic  27.7 us (10%)
  local copies, waits for them, and re-layouts  18.3 us (7%)
  between operations  16.8 us (6%)
    reduce_scatter x2, waiting for transfers between devices, local(): lax.psum_scatter(band_partial, 'col', scatter_dimension=1, tiled=True)  73.7 us
    ppermute x9, starting transfers between devices, padded(): before = lax.ppermute(last, axis, up)  39.6 us
    all_gather x2, blocking collectives, local(): lax.all_gather(band_traces[:, :shard_width], 'row', axis=1, tiled=True)  26.2 us
    all_gather x2, blocking collectives, local(): lax.all_gather(traces.astype(jnp.bfloat16), 'col', axis=1, tiled=True)  21.9 us
    dot_general x2, matrix products, apply_slots(): jnp.einsum('rsk,sjk->srj', col_parts, panel_part, preferred_element_type=...  15.5 us
    add x6, other arithmetic, relax_line(): return (1.0 - JACOBI_WEIGHT) * centre + JACOBI_WEIGHT * gathered / diagonal  15 us
    dot_general x2, matrix products, apply_slots(): jnp.einsum('rsk,skj->srj', row_parts, panel_part, preferred_element_type=...  12.8 us
    ppermute x9, starting transfers between devices, padded(): after = lax.ppermute(first, axis, down)  11.7 us
  transfers between devices with their start and end apart: 22, of which 8 were waited for; matrix products, arithmetic and copies ran while one was open for 21% of the time, Pallas kernels for 0%

commit v1 on v0

v1 whole, which is shorter than its diff:
```python
import functools

import jax
import jax.numpy as jnp
from jax import lax
from jax.experimental import pallas as pl
from jax.experimental.pallas import tpu as pltpu
from jax.sharding import PartitionSpec as P

ITERS = 2
SWEEPS = 4

COUPLING_STEP = 0.3
JACOBI_WEIGHT = 0.8
CELL_MASS = 0.05

LANES = 128
SUB = 8
F32 = jnp.float32
BF16 = jnp.bfloat16


def kernel(
    cfg,
    row_tile_ref,
    col_tile_ref,
    slot_ref,
    surf_ref,
    table_ref,
    start_ref,
    load_ref,
    index_ref,
    source_ref,
    panel_hbm,
    traces_ref,
    response_ref,
    panel,
    own,
    band,
    window,
    edge_left,
    edge_right,
    halo_index,
    halo_source,
    product,
    window_part,
    window_recv,
    row_part,
    row_recv,
    coef_ext,
    source_ext,
    weights,
    state,
    top,
    panel_sem,
    band_send,
    band_recv,
    win_send,
    win_recv,
    edge_send,
    edge_recv,
    halo_send,
    halo_recv,
    part_send,
    part_recv,
    row_send,
    row_rsem,
    band_now,
    window_now,
    edge_now,
):
    cols, rows, lines, per_shard, tile, slots, nodes, layers, rhs, levels = cfg
    dense = cols - lines
    group = cols // lines
    shard = per_shard * tile
    win_tiles = rows * per_shard
    c = lax.axis_index("col")
    r = lax.axis_index("row")
    vol = jnp.maximum(c - dense, 0)
    row_up = jnp.minimum(r + 1, rows - 1)
    row_down = jnp.maximum(r - 1, 0)
    is_volume = c >= dense
    is_dense = c < dense
    first_of_tile = (lax.rem(c, group) == 0) & (r > 0)
    last_of_tile = (lax.rem(c, group) == group - 1) & (r < rows - 1)
    has_left = r > 0
    has_right = r < rows - 1

    def copy(src, dst, send, recv, to_col, to_row):
        return pltpu.make_async_remote_copy(
            src_ref=src,
            dst_ref=dst,
            send_sem=send,
            recv_sem=recv,
            device_id=(to_col, to_row),
            device_id_type=pl.DeviceIdType.MESH,
        )

    def col_peer(k):
        return lax.rem(c + k, cols)

    def row_peer(k):
        return lax.rem(r + k, rows)

    def panel_copy(s):
        return pltpu.make_async_copy(panel_hbm.at[s], panel.at[s], panel_sem.at[s])

    @pl.when(is_dense)
    def _():
        def start(s, _):
            panel_copy(s).start()
            return 0

        lax.fori_loop(0, slots, start, 0)

    barrier = pltpu.get_barrier_semaphore()

    def greet(to_col, to_row):
        pl.semaphore_signal(
            barrier, inc=1, device_id=(to_col, to_row), device_id_type=pl.DeviceIdType.MESH
        )

    for k in range(1, cols):
        greet(col_peer(k), r)
    for k in range(1, rows):
        greet(c, row_peer(k))

    @pl.when(last_of_tile)
    def _():
        for v in range(lines):
            greet(dense + v, row_up)

    @pl.when(first_of_tile)
    def _():
        for v in range(lines):
            greet(dense + v, row_down)

    @pl.when(is_volume & has_left)
    def _():
        for q in range(lines):
            greet(q * group + group - 1, row_down)

    @pl.when(is_volume & has_right)
    def _():
        for q in range(lines):
            greet(q * group, row_up)

    def count(flag):
        return jnp.where(flag, lines, 0)

    expected = (
        cols
        - 1
        + rows
        - 1
        + count(last_of_tile)
        + count(first_of_tile)
        + count(is_volume & has_left)
        + count(is_volume & has_right)
    )
    traces_ref[...] = start_ref[...]
    product[slots] = jnp.zeros((rhs, tile), F32)
    pl.semaphore_wait(barrier, expected)

    def halo_copy(kind, side, arrival=False):
        ref = (index_ref, source_ref)[kind]
        dst = (halo_index, halo_source)[kind]
        at = nodes - LANES if side == 0 else 0
        to = row_up if (side == 0) != arrival else row_down
        return copy(
            ref.at[:, :, pl.ds(at, LANES)],
            dst.at[side],
            halo_send.at[kind, side],
            halo_recv.at[kind, side],
            c,
            to,
        )

    sides = ((0, has_right, has_left), (1, has_left, has_right))
    for side, sends, _ in sides:

        @pl.when(is_volume & sends)
        def _():
            for kind in range(2):
                halo_copy(kind, side).start()

    def band_copy(it, k):
        to = col_peer(k)
        return copy(own.at[it], band.at[it, c], band_send.at[it, k], band_recv.at[it, c], to, r)

    def band_arrival(it, src):
        return copy(own.at[it], band.at[it, src], band_send.at[it, 0], band_recv.at[it, src], src, r)

    def edge_copy(it, side, v):
        q = lax.div(c, group)
        if side == 0:
            src = own.at[it, per_shard - 1, :, pl.ds(tile - LANES, LANES)]
            dst, to = edge_left, row_up
        else:
            src = own.at[it, 0, :, pl.ds(0, LANES)]
            dst, to = edge_right, row_down
        return copy(
            src,
            dst.at[it, q],
            edge_send.at[it, side, v],
            edge_recv.at[it, side, q],
            dense + v,
            to,
        )

    def edge_arrival(it, side, q):
        dst = (edge_left, edge_right)[side]
        src = own.at[it, 0, :, pl.ds(0, LANES)]
        if side == 0:
            from_col, from_row = q * group + group - 1, row_down
        else:
            from_col, from_row = q * group, row_up
        return copy(
            src,
            dst.at[it, q],
            edge_send.at[it, side, 0],
            edge_recv.at[it, side, q],
            from_col,
            from_row,
        )

    def window_copy(it, k):
        to = row_peer(k)
        return copy(band.at[it, 0], window.at[it, r], win_send.at[it, k], win_recv.at[it, r], c, to)

    def window_arrival(it, k):
        src = row_peer(k)
        return copy(
            band.at[it, 0], window.at[it, src], win_send.at[it, k], win_recv.at[it, src], c, src
        )

    def part_copy(it, k):
        to = row_peer(k)
        return copy(
            window_part.at[it, to],
            window_recv.at[it, r],
            part_send.at[it, k],
            part_recv.at[it, r],
            c,
            to,
        )

    def part_arrival(it, k):
        src = row_peer(k)
        return copy(
            window_part.at[it, src],
            window_recv.at[it, src],
            part_send.at[it, k],
            part_recv.at[it, src],
            c,
            src,
        )

    def row_copy(it, to):
        return copy(
            row_part.at[it, to], row_recv.at[it, c], row_send.at[it, to], row_rsem.at[it, c], to, r
        )

    def row_arrival(it, src):
        return copy(
            row_part.at[it, src],
            row_recv.at[it, src],
            row_send.at[it, src],
            row_rsem.at[it, src],
            src,
            r,
        )

    def prepare_volume():
        line = lax.div(surf_ref[r * lines + vol], rows)
        padded = nodes + 4 * LANES
        for side, _, receives in sides:

            @pl.when(receives)
            def _():
                for kind in range(2):
                    halo_copy(kind, side, True).wait_recv()

            @pl.when(jnp.logical_not(receives))
            def _():
                halo_index[side] = jnp.zeros((lines, layers, LANES), jnp.int32)
                halo_source[side] = jnp.zeros((lines, layers, LANES), F32)

        def lookup(indices):
            values = jnp.zeros(indices.shape, F32)
            for level in range(levels):
                values = jnp.where(indices == level, table_ref[level], values)
            return values

        zeros = jnp.zeros((layers, LANES), F32)
        left_on = jnp.where(has_left, 1.0, 0.0)
        right_on = jnp.where(has_right, 1.0, 0.0)
        right_at = 2 * LANES + nodes
        coef_ext[:, 0:LANES] = zeros
        coef_ext[:, LANES : 2 * LANES] = lookup(halo_index[0, line]) * left_on
        coef_ext[:, 2 * LANES : right_at] = lookup(index_ref[line])
        coef_ext[:, right_at : right_at + LANES] = lookup(halo_index[1, line]) * right_on
        coef_ext[:, right_at + LANES :] = zeros
        source_ext[:, 0:LANES] = zeros
        source_ext[:, LANES : 2 * LANES] = halo_source[0, line]
        source_ext[:, 2 * LANES : right_at] = source_ref[line]
        source_ext[:, right_at : right_at + LANES] = halo_source[1, line]
        source_ext[:, right_at + LANES :] = zeros
        lane = lax.broadcasted_iota(jnp.int32, (1, padded), 1)
        low = jnp.where(has_left, LANES, 2 * LANES)
        high = jnp.where(has_right, right_at + LANES, right_at)
        inside = (lane >= low) & (lane < high)
        for layer in range(layers):
            k = coef_ext[layer : layer + 1, :]
            left = 0.5 * (k + pltpu.roll(k, 1, 1))
            right = 0.5 * (k + pltpu.roll(k, padded - 1, 1))
            up = 0.5 * (k + coef_ext[layer - 1 : layer, :]) if layer else k
            diagonal = left + right + up + CELL_MASS
            parts = [left, right, up]
            if layer < layers - 1:
                down = 0.5 * (k + coef_ext[layer + 1 : layer + 2, :])
                diagonal = diagonal + down
                parts.append(down)
            else:
                parts.append(None)
            parts.append(source_ext[layer : layer + 1, :])
            scale = jnp.where(inside, JACOBI_WEIGHT / diagonal, 0.0)
            for kind, part in enumerate(parts):
                if part is not None:
                    weights[kind, layer] = jnp.broadcast_to(part * scale, (SUB, padded))
        top[:, 0:LANES] = jnp.zeros((rhs, LANES), F32)
        top[:, right_at + LANES :] = jnp.zeros((rhs, LANES), F32)
        for layer in range(layers):
            state[0, layer] = jnp.zeros((rhs, padded), F32)
            state[1, layer, :, 0:LANES] = jnp.zeros((rhs, LANES), F32)
            state[1, layer, :, right_at + LANES :] = jnp.zeros((rhs, LANES), F32)

    def relax(now, at, width):
        span = width + 2 * LANES
        begin = pl.multiple_of(at - LANES, LANES)
        at = pl.multiple_of(at, LANES)
        for layer in range(layers):
            factors = [
                None if kind == 3 and layer == layers - 1 else weights[kind, layer, :, pl.ds(at, width)]
                for kind in range(5)
            ]
            for g in range(rhs // SUB):
                lines_at = pl.ds(g * SUB, SUB)
                around = state[now, layer, lines_at, pl.ds(begin, span)]
                centre = around[:, LANES : LANES + width]
                before = pltpu.roll(around, 1, 1)[:, LANES : LANES + width]
                after = pltpu.roll(around, span - 1, 1)[:, LANES : LANES + width]
                if layer:
                    above = state[now, layer - 1, lines_at, pl.ds(at, width)]
                else:
                    above = top[lines_at, pl.ds(at, width)]
                value = (1.0 - JACOBI_WEIGHT) * centre + factors[4]
                value = value + factors[0] * before + factors[1] * after + factors[2] * above
                if layer < layers - 1:
                    value = value + factors[3] * state[now, layer + 1, lines_at, pl.ds(at, width)]
                state[1 - now, layer, lines_at, pl.ds(at, width)] = value

    def volume(it):
        q = vol
        right_at = 2 * LANES + nodes
        for m in range(group):
            src = q * group + m

            @pl.when(src != c)
            def _():
                band_arrival(it, src).wait_recv()

            for p in range(per_shard):
                at = 2 * LANES + m * shard + p * tile
                top[:, at : at + tile] = band[it, src, p].astype(F32)
        line = lax.div(surf_ref[r * lines + q], rows)
        for side, _, receives in sides:
            dst = (edge_left, edge_right)[side]
            at = LANES if side == 0 else right_at
            base = row_down if side == 0 else row_up
            place = 0
            for z in range(lines):
                place = jnp.where(surf_ref[base * lines + z] == line * rows + base, z, place)

            @pl.when(receives)
            def _():
                for z in range(lines):
                    edge_arrival(it, side, z).wait_recv()
                for z in range(lines):
                    edge_now[z] = dst[it, z]
                top[:, at : at + LANES] = edge_now[place].astype(F32)

            @pl.when(jnp.logical_not(receives))
            def _():
                top[:, at : at + LANES] = jnp.zeros((rhs, LANES), F32)

        def sweep(i, _):
            now = lax.rem(i, 2)
            relax(now, LANES, LANES)
            relax(now, right_at, LANES)

            def chunk(j, _):
                relax(now, 2 * LANES + j * tile, tile)
                return 0

            lax.fori_loop(0, nodes // tile, chunk, 0)
            return 0

        lax.fori_loop(0, SWEEPS, sweep, 0)
        done = SWEEPS % 2
        for m in range(group):
            to = q * group + m
            for p in range(per_shard):
                at = 2 * LANES + m * shard + p * tile
                k = index_coef(at)
                flux = k * (top[:, at : at + tile] - state[done, 0, :, at : at + tile])
                row_part[it, to, p] = flux.astype(BF16)

            @pl.when(to != c)
            def _():
                row_copy(it, to).start()

    def index_coef(at):
        return coef_ext[0:1, at : at + tile]

    def total_of(tiles_of):
        value = product[tiles_of[0]]
        for t in tiles_of[1:]:
            value = value + product[t]
        return value

    def dense_part(it):
        @pl.when(c != 0)
        def _():
            band_arrival(it, 0).wait_recv()

        for k in range(1, rows):
            window_copy(it, k).start()
        window[it, r] = band[it, 0]
        for src in range(1, cols):

            @pl.when(c != src)
            def _():
                band_arrival(it, src).wait_recv()

        for src in range(cols):
            band_now[src] = band[it, src]

        def into_cols(s, _):
            @pl.when(it == 0)
            def _():
                panel_copy(s).wait()

            row_tile = row_tile_ref[s]
            traces = band_now[lax.div(row_tile, per_shard), lax.rem(row_tile, per_shard)]
            product[s] = jnp.dot(traces, panel[s], preferred_element_type=F32)
            return 0

        lax.fori_loop(0, slots, into_cols, 0)
        band_tiles = cols * per_shard

        def sum_window(j, _):
            value = total_of([slot_ref[b * win_tiles + j] for b in range(band_tiles)])
            window_part[it, lax.div(j, per_shard), lax.rem(j, per_shard)] = value.astype(BF16)
            return 0

        lax.fori_loop(0, win_tiles, sum_window, 0)
        for k in range(1, rows):
            part_copy(it, k).start()
        for k in range(1, rows):
            window_arrival(it, k).wait_recv()

        for src in range(rows):
            window_now[src] = window[it, src]

        def into_rows(s, _):
            col_tile = col_tile_ref[s]
            traces = window_now[lax.div(col_tile, per_shard), lax.rem(col_tile, per_shard)]
            product[s] = lax.dot_general(
                traces, panel[s], (((1,), (1,)), ((), ())), preferred_element_type=F32
            )
            return 0

        lax.fori_loop(0, slots, into_rows, 0)

        def sum_rows(b, _):
            value = total_of([slot_ref[b * win_tiles + j] for j in range(win_tiles)])
            row_part[it, lax.div(b, per_shard), lax.rem(b, per_shard)] = value.astype(BF16)
            return 0

        lax.fori_loop(per_shard, band_tiles, sum_rows, 0)
        for to in range(1, cols):

            @pl.when(c != to)
            def _():
                row_copy(it, to).start()

        for k in range(1, rows):
            part_arrival(it, k).wait_recv()
        for p in range(per_shard):
            value = total_of([slot_ref[p * win_tiles + j] for j in range(win_tiles)])
            value = value + window_part[it, r, p].astype(F32)
            for k in range(1, rows):
                value = value + window_recv[it, row_peer(k), p].astype(F32)
            row_part[it, 0, p] = value.astype(BF16)

        @pl.when(c != 0)
        def _():
            row_copy(it, 0).start()

    def iteration(it, _):
        for p in range(per_shard):
            rounded = traces_ref[:, p * tile : (p + 1) * tile].astype(BF16)
            own[it, p] = rounded
            band[it, c, p] = rounded
        for k in range(1, cols):
            band_copy(it, k).start()
        for side, flag in ((0, last_of_tile), (1, first_of_tile)):

            @pl.when(flag)
            def _():
                for v in range(lines):
                    edge_copy(it, side, v).start()

        @pl.when(is_volume)
        def _():
            @pl.when(it == 0)
            def _():
                prepare_volume()

            volume(it)
            for k in range(cols):

                @pl.when((k != c) & (k // group != c - dense))
                def _():
                    band_arrival(it, k).wait_recv()

        @pl.when(is_dense)
        def _():
            dense_part(it)

        owner = dense + lax.div(c, group)
        for src in range(cols):

            @pl.when((src != c) & ((src < dense) | (src == owner)))
            def _():
                row_arrival(it, src).wait_recv()

        def own_part(p):
            return row_part[it, c, p].astype(F32)

        for p in range(per_shard):
            at = slice(p * tile, (p + 1) * tile)
            response_ref[:, at] = jnp.zeros((rhs, tile), F32)
            for src in range(dense):

                @pl.when(src != c)
                def _():
                    response_ref[:, at] += row_recv[it, src, p].astype(F32)

            @pl.when(owner != c)
            def _():
                response_ref[:, at] += row_recv[it, owner, p].astype(F32)

            @pl.when(is_dense | (owner == c))
            def _():
                response_ref[:, at] += own_part(p)

            t = traces_ref[:, at]
            traces_ref[:, at] = t + COUPLING_STEP * (load_ref[:, at] - t - response_ref[:, at])
        return 0

    lax.fori_loop(0, ITERS, iteration, 0)

    def drain(it, _):
        for k in range(1, cols):
            band_copy(it, k).wait_send()
        for side, flag in ((0, last_of_tile), (1, first_of_tile)):

            @pl.when(flag)
            def _():
                for v in range(lines):
                    edge_copy(it, side, v).wait_send()

        @pl.when(is_dense)
        def _():
            for k in range(1, rows):
                window_copy(it, k).wait_send()
                part_copy(it, k).wait_send()
            for to in range(cols):

                @pl.when(c != to)
                def _():
                    row_copy(it, to).wait_send()

        @pl.when(is_volume)
        def _():
            for m in range(group):
                to = vol * group + m

                @pl.when(to != c)
                def _():
                    row_copy(it, to).wait_send()

        return 0

    lax.fori_loop(0, ITERS, drain, 0)
    for side, sends, _ in sides:

        @pl.when(is_volume & sends)
        def _():
            for kind in range(2):
                halo_copy(kind, side).wait_send()


def local(
    trace_start, surface_load, panel_tiles, tile_list, surf_map, coef_index, coef_table, vol_source
):
    cols = lax.axis_size("col")
    rows = lax.axis_size("row")
    row_index = lax.axis_index("row")
    lines, layers, nodes = coef_index.shape
    slots, tile, _ = panel_tiles.shape
    rhs, shard = trace_start.shape
    per_shard = shard // tile
    levels = coef_table.shape[0]
    side = cols * rows * per_shard
    band_tiles = cols * per_shard
    win_tiles = rows * per_shard
    safe = jnp.maximum(tile_list, 0)
    row_tile = safe // side
    col_tile = safe % side
    band_tile = row_tile // per_shard // rows * per_shard + row_tile % per_shard
    b = jnp.arange(band_tiles, dtype=jnp.int32)
    name_row = (b // per_shard * rows + row_index) * per_shard + b % per_shard
    names = (name_row[:, None] * side + jnp.arange(win_tiles, dtype=jnp.int32)).reshape(-1)
    order = jnp.arange(slots, dtype=jnp.int32)
    slot_table = slots - jnp.max(
        jnp.where(names[:, None] == tile_list[None, :], slots - order, 0), axis=1
    )
    padded = nodes + 4 * LANES
    cfg = (cols, rows, lines, per_shard, tile, slots, nodes, layers, rhs, levels)
    smem = pl.BlockSpec(memory_space=pltpu.SMEM)
    vmem = pl.BlockSpec(memory_space=pltpu.VMEM)
    block = (per_shard, rhs, tile)
    dma = pltpu.SemaphoreType.DMA
    out = jax.ShapeDtypeStruct((rhs, shard), F32)
    return pl.pallas_call(
        functools.partial(kernel, cfg),
        out_shape=(out, out),
        in_specs=[smem] * 5 + [vmem] * 4 + [pl.BlockSpec(memory_space=pl.ANY)],
        out_specs=(vmem, vmem),
        scratch_shapes=[
            pltpu.VMEM((slots, tile, tile), BF16),
            pltpu.VMEM((ITERS,) + block, BF16),
            pltpu.VMEM((ITERS, cols) + block, BF16),
            pltpu.VMEM((ITERS, rows) + block, BF16),
            pltpu.VMEM((ITERS, lines, rhs, LANES), BF16),
            pltpu.VMEM((ITERS, lines, rhs, LANES), BF16),
            pltpu.VMEM((2, lines, layers, LANES), jnp.int32),
            pltpu.VMEM((2, lines, layers, LANES), F32),
            pltpu.VMEM((slots + 1, rhs, tile), F32),
            pltpu.VMEM((ITERS, rows) + block, BF16),
            pltpu.VMEM((ITERS, rows) + block, BF16),
            pltpu.VMEM((ITERS, cols) + block, BF16),
            pltpu.VMEM((ITERS, cols) + block, BF16),
            pltpu.VMEM((layers, padded), F32),
            pltpu.VMEM((layers, padded), F32),
            pltpu.VMEM((5, layers, SUB, padded), F32),
            pltpu.VMEM((2, layers, rhs, padded), F32),
            pltpu.VMEM((rhs, padded), F32),
            dma((slots,)),
            dma((ITERS, cols)),
            dma((ITERS, cols)),
            dma((ITERS, rows)),
            dma((ITERS, rows)),
            dma((ITERS, 2, lines)),
            dma((ITERS, 2, lines)),
            dma((2, 2)),
            dma((2, 2)),
            dma((ITERS, rows)),
            dma((ITERS, rows)),
            dma((ITERS, cols)),
            dma((ITERS, cols)),
            pltpu.VMEM((cols,) + block, BF16),
            pltpu.VMEM((rows,) + block, BF16),
            pltpu.VMEM((lines, rhs, LANES), BF16),
        ],
        compiler_params=pltpu.CompilerParams(
            collective_id=0, has_side_effects=True, vmem_limit_bytes=60 * 1024 * 1024
        ),
        name="coupled",
    )(
        band_tile,
        col_tile,
        slot_table,
        surf_map,
        coef_table,
        trace_start,
        surface_load,
        coef_index,
        vol_source,
        panel_tiles,
    )


def solution(mesh):
    return jax.shard_map(
        local,
        mesh=mesh,
        in_specs=(
            P(None, ("col", "row")),
            P(None, ("col", "row")),
            P(("col", "row"), None, None),
            P(("col", "row")),
            P(),
            P(None, None, "row"),
            P(),
            P(None, None, "row"),
        ),
        out_specs=(P(None, ("col", "row")), P(None, ("col", "row"))),
        check_vma=False,
    )
```

time: 280 us -> 124 us (0.44)
  Pallas kernels: 0 us -> 118 us
  waiting for transfers between devices: 79 us -> 0 us
  starting transfers between devices: 51.5 us -> 0 us
  blocking collectives: 48.1 us -> 0 us
  matrix products: 36.5 us -> 0 us
  other arithmetic: 27.7 us -> 2.6 us
  between operations: 16.8 us -> 0.66 us
  local copies, waits for them, and re-layouts: 18.3 us -> 3.22 us
    pallas_call x0 -> x1, Pallas kernels: none -> 118 us  [local(): pl.pallas_call(functools.partial(kernel, cfg), out_shape=(out, out), in_s...]
    reduce_scatter x4 -> x0, waiting for transfers between devices: 73.7 us -> none  [the longest x2 73.7 us: local(): lax.psum_scatter(band_partial, 'col', scatter_dimension=1, tiled=True)]
    ppermute x18 -> x0, starting transfers between devices: 51.4 us -> none  [the longest x9 39.6 us: padded(): before = lax.ppermute(last, axis, up)]
    all_gather x4 -> x0, blocking collectives: 48.1 us -> none  [the longest x2 26.2 us: local(): lax.all_gather(band_traces[:, :shard_width], 'row', axis=1, tiled=True)]
    dot_general x8 -> x0, matrix products: 36.5 us -> none  [the longest x2 15.5 us: apply_slots(): jnp.einsum('rsk,sjk->srj', col_parts, panel_part, preferred_element_type=...]
    add x9 -> x1, other arithmetic: 17.9 us -> 0.07 us  [local(): name_row[:, None] * side + jnp.arange(win_tiles, dtype=jnp.int32)]
    slice x23 -> x0, local copies, waits for them, and re-layouts: 8.97 us -> none  [the longest x6 5.48 us: relax_line(): centre[:, 1:]]
    ppermute x18 -> x0, waiting for transfers between devices: 5.2 us -> none  [the longest x9 5.08 us: padded(): before = lax.ppermute(last, axis, up)]
  transfers between devices with their start and end apart: 22 -> 0, of which waited for: 8 -> 0; matrix products, arithmetic and copies ran while one was open for 21% -> 0% of each run, Pallas kernels for 0% -> 0%
where the time goes in v1:
time: 124 us
  Pallas kernels  118 us (95%)
  local copies, waits for them, and re-layouts  3.22 us (3%)
  other arithmetic  2.6 us (2%)
    pallas_call x1, Pallas kernels, local(): pl.pallas_call(functools.partial(kernel, cfg), out_shape=(out, out), in_s...  118 us
    unnamed x2, local copies, waits for them, and re-layouts  3.14 us

profile of v1, /device:TPU:1, one launch (start us, length us, event | category | flops | bytes accessed | tf_op | source)
XLA Modules:
  0.0 124.1 jit_solution(8406375403076187054)
XLA Ops:
  0.7 1.2 and_select_fusion.2
  1.8 0.1 iota_add_fusion
  1.9 0.1 add.78
  2.0 0.7 select_reduce_fusion
  2.8 0.6 broadcast_subtract_fusion.slot_ref
  3.3 117.6 %coupled.1 = (f32[32,1024]{1,0:T(8,128)}, f32[32,1024]{1,0:T(8,128)}) custom-call(s32[22]{0:T(128)} %get-tuple-element.3.row_tile_ref, s32[22]{0:T(128)} %get-tuple-element.2.col_tile_ref, s32[128]{0:T(128)} %broadcast_subtract_fusion.slot_ref, s32[8]{0:T(128)} %surf_ref.1, f32[16]{0:T(128)} %table_ref.1, f32[32,1024]{1,0:T(8,128)} %start_ref.1, ...), custom_call_target="tpu_custom_call" | custom-call | tf_op jit(solution)/shard_map/coupled/pallas_call | solution.py:648
  120.9 1.6 %copy.12 = f32[32,1024]{1,0:T(8,128)} copy(f32[32,1024]{1,0:T(8,128)} %get-tuple-element.6) | data formatting | bytes 262144
  122.5 1.6 %copy.13 = f32[32,1024]{1,0:T(8,128)} copy(f32[32,1024]{1,0:T(8,128)} %get-tuple-element.7) | data formatting | bytes 262144
  (2 shorter events, 0.0 us)

commit v2 on v1

--- a/solution.py
+++ b/solution.py
@@ -394,19 +394,20 @@
             def _():
                 top[:, at : at + LANES] = jnp.zeros((rhs, LANES), F32)
 
-        def sweep(i, _):
-            now = lax.rem(i, 2)
+        width = 2 * tile
+
+        def sweep(now):
             relax(now, LANES, LANES)
             relax(now, right_at, LANES)
 
             def chunk(j, _):
-                relax(now, 2 * LANES + j * tile, tile)
+                relax(now, 2 * LANES + j * width, width)
                 return 0
 
-            lax.fori_loop(0, nodes // tile, chunk, 0)
-            return 0
-
-        lax.fori_loop(0, SWEEPS, sweep, 0)
+            lax.fori_loop(0, nodes // width, chunk, 0)
+
+        for i in range(SWEEPS):
+            sweep(i % 2)
         done = SWEEPS % 2
         for m in range(group):
             to = q * group + m

time: 124 us -> 86.4 us (0.70)
  Pallas kernels: 118 us -> 79.7 us
    pallas_call x1, Pallas kernels: 118 us -> 79.7 us  [local(): pl.pallas_call(functools.partial(kernel, cfg), out_shape=(out, out), in_s...]
where the time goes in v2:
time: 86.4 us; the launch traced here: 86.2 us
  Pallas kernels  79.7 us (92%)
  local copies, waits for them, and re-layouts  3.22 us (4%)
  other arithmetic  2.6 us (3%)
    pallas_call x1, Pallas kernels, local(): pl.pallas_call(functools.partial(kernel, cfg), out_shape=(out, out), in_s...  79.7 us
    unnamed x2, local copies, waits for them, and re-layouts  3.14 us

profile of v2, /device:TPU:1, one launch (start us, length us, event | category | flops | bytes accessed | tf_op | source)
XLA Modules:
  0.0 86.2 jit_solution(3795848848002160535)
XLA Ops:
  0.7 1.2 %and_select_fusion.2 = (s32[22]{0:T(128)}, s32[22]{0:T(128)}) fusion(s32[22]{0:T(128)} %param.11), kind=kLoop, calls=%fused_computation.4 | loop fusion | flops 1078 | bytes 264 | tf_op jit(solution)/shard_map/jit(remainder)/select_n | solution.py:633
  1.8 0.1 iota_add_fusion
  1.9 0.1 add.78
  2.0 0.7 select_reduce_fusion
  2.8 0.6 broadcast_subtract_fusion.slot_ref
  3.3 79.7 %coupled.1 = (f32[32,1024]{1,0:T(8,128)}, f32[32,1024]{1,0:T(8,128)}) custom-call(s32[22]{0:T(128)} %get-tuple-element.3.row_tile_ref, s32[22]{0:T(128)} %get-tuple-element.2.col_tile_ref, s32[128]{0:T(128)} %broadcast_subtract_fusion.slot_ref, s32[8]{0:T(128)} %surf_ref.1, f32[16]{0:T(128)} %table_ref.1, f32[32,1024]{1,0:T(8,128)} %start_ref.1, ...), custom_call_target="tpu_custom_call" | custom-call | tf_op jit(solution)/shard_map/coupled/pallas_call | solution.py:649
  83.1 1.6 %copy.12 = f32[32,1024]{1,0:T(8,128)} copy(f32[32,1024]{1,0:T(8,128)} %get-tuple-element.6) | data formatting | bytes 262144
  84.6 1.6 %copy.13 = f32[32,1024]{1,0:T(8,128)} copy(f32[32,1024]{1,0:T(8,128)} %get-tuple-element.7) | data formatting | bytes 262144
  (2 shorter events, 0.0 us)
